TPU v7x, 256 devices: a whole 4x4x8 slice. The times are simulated.
256 devices in a mesh: shift: 4 (over y_lo, core), band: 4 (over z_lo), lane: 16 (over z_hi, y_hi, x).
Axes of the slice: x: 4, y: 4 (y_hi: 2, y_lo: 2; y = y_hi * 2 + y_lo), z: 8 (z_hi: 2, z_lo: 4; z = z_hi * 4 + z_lo), core: 2. Of those that a mesh axis runs over, the one named last changes fastest.
Arguments:
- source_terms: float32 [1024, 1024, 128], P(('shift', 'band'), 'lane'), parts along dimension 0, may hold values from -6 to 6
- initial_values: float32 [1024, 1024, 128], P(('shift', 'band'), 'lane'), parts along dimension 0, may hold values from -6 to 6
- absorption: float32 [1024, 1024, 128], P(('shift', 'band'), 'lane'), parts along dimension 0, may hold values from 0.1 to 0.9
Outputs:
- corrected: float32 [1024, 1024, 128], P(('shift', 'band'), 'lane'), parts along dimension 0
There are 4 independent parts, one for each index of `shift`. A program takes and returns all parts, laid end to end along the dimension named above; each array names one. Nothing has to cross between parts.
All inputs are finite; a program needn't handle non-finite values.
Results may differ from a plain program's by a relative error of at most 0.0003.
Values sent between devices are 32-bit elements.
A program may use at most 64 MiB of HBM per device.

v0:
```python
import functools

import jax
import jax.numpy as jnp
from jax import lax
from jax.experimental import pallas as pl
from jax.experimental.pallas import tpu as pltpu
from jax.sharding import PartitionSpec as P

RATIO = 2
BEFORE = 3
AFTER = 3
INNER = 13
HALO = 8
ROWS = 2
SUB = 8
MESH = pl.DeviceIdType.MESH
CHUNKS = 4
BLOCK = 8
DIRS = [(-1, 0), (1, 0), (0, -1), (0, 1), (-1, -1), (-1, 1), (1, -1), (1, 1)]

TRADES = [
    ("u_first", "fine", 2),
    ("w", "fine", 1),
    ("f", "fine", 1),
    ("cw", "coarse", 6),
    ("u_second", "fine", 2),
    ("cf", "coarse", 7),
    ("cu", "coarse", 6),
    ("u_third", "fine", 2),
]


class Grid:
    def __init__(self, rows, columns, row_halo, column_halo):
        self.rows, self.columns = rows, columns
        self.row_halo, self.column_halo = row_halo, column_halo
        self.pieces = (columns + 2 * column_halo) // SUB
        self.width = self.pieces * SUB
        self.stored = (rows + 2 * row_halo) * self.width

    def at(self, column):
        return (column % self.pieces) * SUB + column // self.pieces


def kernel(grids, src_hbm, init_hbm, abs_hbm, out_hbm, *scratch):
    fine, coarse = grids["fine"], grids["coarse"]
    raw = scratch[:3]
    u, v, w, f, iw, out, cw, cf, ca, cb, in_sem, out_sem, send_sem, recv_sem = scratch[3:17]
    lands = scratch[17:]
    band, lane = lax.axis_index("band"), lax.axis_index("lane")
    bands, lanes = lax.axis_size("band"), lax.axis_size("lane")

    def exists(q):
        dy, dx = q
        there = jnp.bool_(True)
        if dy:
            there = (band > 0) if dy < 0 else (band < bands - 1)
        if dx:
            beside = (lane > 0) if dx < 0 else (lane < lanes - 1)
            there = beside if not dy else there & beside
        return there

    def name_of(q):
        return {"band": band + q[0], "lane": lane + q[1]}

    loads = [
        pltpu.make_async_copy(
            ref,
            raw[i].reshape(fine.rows, fine.width, 128).at[:, pl.ds(fine.column_halo, fine.columns), :],
            in_sem.at[i],
        )
        for i, ref in enumerate((abs_hbm, src_hbm, init_hbm))
    ]
    for i in (2, 0, 1):
        loads[i].start()

    trades = {}
    for t, (name, which, depth) in enumerate(TRADES):
        trades[name] = (t, grids[which], depth) + tuple(lands[5 * t : 5 * t + 5])

    barrier = pltpu.get_barrier_semaphore()
    for q in DIRS:
        @pl.when(exists(q))
        def _():
            pl.semaphore_signal(barrier, inc=1, device_id=name_of(q), device_id_type=MESH)

    def landing(trade, q):
        t, g, depth, sides, strips, rows, columns, corners = trade
        dy, dx = q
        if not dx:
            return rows.at[(dy + 1) // 2, :, pl.ds(g.column_halo, g.columns), :]
        if not dy:
            return columns.at[(dx + 1) // 2]
        return corners.at[(dy + 1) // 2 * 2 + (dx + 1) // 2]

    def source(trade, q):
        t, g, depth, sides, strips, rows, columns, corners = trade
        dy, dx = q
        if not dx:
            return sides.at[(dy + 1) // 2, :, pl.ds(g.column_halo, g.columns), :]
        strip = strips.at[(dx + 1) // 2]
        if not dy:
            return strip
        return strip.at[:, pl.ds(0 if dy < 0 else g.rows - SUB, SUB), :]

    for trade in trades.values():
        for q in DIRS:
            @pl.when(jnp.logical_not(exists(q)))
            def _():
                ref = landing(trade, q)
                ref[...] = jnp.zeros(ref.shape, jnp.float32)

    on_band = (band > 0).astype(jnp.int32) + (band < bands - 1).astype(jnp.int32)
    on_lane = (lane > 0).astype(jnp.int32) + (lane < lanes - 1).astype(jnp.int32)
    pl.semaphore_wait(barrier, (on_band + 1) * (on_lane + 1) - 1)

    def copy_of(trade, q, arriving):
        t = trade[0]
        back = (-q[0], -q[1])
        i, j = DIRS.index(q), DIRS.index(back)
        return pltpu.make_async_remote_copy(
            src_ref=source(trade, q if not arriving else back),
            dst_ref=landing(trade, back if not arriving else q),
            send_sem=send_sem.at[t * 8 + i],
            recv_sem=recv_sem.at[t * 8 + (i if arriving else j)],
            device_id=name_of(q),
            device_id_type=MESH,
        )

    def start(trade, directions):
        for q in directions:
            @pl.when(exists(q))
            def _():
                copy_of(trade, q, False).start()

    def send(name, arr):
        trade = trades[name]
        t, g, depth, sides, strips, rows, columns, corners = trade
        for side in range(2):
            first = g.column_halo if side == 0 else g.column_halo + g.columns - depth
            for j in range(depth):
                for i in range(g.rows // SUB):
                    at = (g.row_halo + SUB * i) * g.width + g.at(first + j)
                    strips[side, j, pl.ds(SUB * i, SUB), :] = arr[
                        pl.ds(at, SUB, stride=g.width), :
                    ]
        start(trade, DIRS[4:])
        start(trade, DIRS[2:4])
        for side in range(2):
            first = g.row_halo if side == 0 else g.row_halo + g.rows - depth
            for i in range(depth):
                for k in range(g.pieces):
                    sides[side, i, pl.ds(k, SUB, stride=g.pieces), :] = piece(arr, g, first + i, k)
        start(trade, DIRS[:2])

    def send_raw(name, value):
        trade = trades[name]
        t, g, depth, sides, strips, rows, columns, corners = trade
        for side in range(2):
            first = g.column_halo if side == 0 else g.column_halo + g.columns - depth
            for j in range(depth):
                for i in range(g.rows // SUB):
                    strips[side, j, pl.ds(SUB * i, SUB), :] = value(
                        lambda ref: ref[pl.ds(SUB * i * g.width + first + j, SUB, stride=g.width), :]
                    )
        start(trade, DIRS[4:])
        start(trade, DIRS[2:4])
        for side in range(2):
            first = 0 if side == 0 else g.rows - depth
            for i in range(depth):
                for c in range(g.columns // SUB):
                    at = g.column_halo + SUB * c
                    sides[side, i, pl.ds(at, SUB), :] = value(
                        lambda ref: ref[pl.ds((first + i) * g.width + at, SUB), :]
                    )
        start(trade, DIRS[:2])

    def receive(name, arr):
        trade = trades[name]
        t, g, depth, sides, strips, rows, columns, corners = trade
        for q in DIRS:
            @pl.when(exists(q))
            def _():
                copy_of(trade, q, False).wait_send()
                copy_of(trade, q, True).wait_recv()
        for side in range(2):
            first = g.row_halo - depth if side == 0 else g.row_halo + g.rows
            for i in range(depth):
                for k in range(g.pieces):
                    put(arr, g, first + i, k, rows[side, i, pl.ds(k, SUB, stride=g.pieces), :])
        for side in range(2):
            first = g.column_halo - depth if side == 0 else g.column_halo + g.columns
            for j in range(depth):
                place = g.at(first + j)
                for i in range(g.rows // SUB):
                    at = (g.row_halo + SUB * i) * g.width + place
                    arr[pl.ds(at, SUB, stride=g.width), :] = columns[
                        side, j, pl.ds(SUB * i, SUB), :
                    ]
                for end in range(2):
                    row = g.row_halo - depth if end == 0 else g.row_halo + g.rows
                    skip = SUB - depth if end == 0 else 0
                    arr[pl.ds(row * g.width + place, depth, stride=g.width), :] = corners[
                        end * 2 + side, j, pl.ds(skip, depth), :
                    ]

    def piece(ref, g, row, k):
        return ref[pl.ds(pl.multiple_of(row * g.width + k * SUB, SUB), SUB), :]

    def put(ref, g, row, k, value):
        ref[pl.ds(pl.multiple_of(row * g.width + k * SUB, SUB), SUB), :] = value

    def around(ref, g, row):
        here = [piece(ref, g, row, k) for k in range(g.pieces)]
        before = [pltpu.roll(here[-1], 1, 0)] + here[:-1]
        after = here[1:] + [pltpu.roll(here[0], SUB - 1, 0)]
        sums = [
            (piece(ref, g, row - 1, k) + piece(ref, g, row + 1, k)) + (before[k] + after[k])
            for k in range(g.pieces)
        ]
        return here, sums

    def block(g, old, new, weight, load, row, count, ks):
        seen = {}

        def get(i, k):
            if (i, k) not in seen:
                seen[i, k] = piece(old, g, row + i, k)
            return seen[i, k]

        for k in ks:
            for i in range(count):
                left = get(i, k - 1) if k else pltpu.roll(get(i, g.pieces - 1), 1, 0)
                right = get(i, k + 1) if k < g.pieces - 1 else pltpu.roll(get(i, 0), SUB - 1, 0)
                total = (get(i - 1, k) + get(i + 1, k)) + (left + right)
                value = (
                    0.2 * get(i, k)
                    + piece(load, g, row + i, k)
                    + piece(weight, g, row + i, k) * total
                )
                if new is out:
                    at = (row + i - g.row_halo) * g.width + k
                    new[pl.ds(at, SUB, stride=g.pieces), :] = value
                else:
                    put(new, g, row + i, k, value)

    def part(g, old, new, weight, load, first, last, ks):
        whole = (last - first) // BLOCK

        @pl.loop(0, whole)
        def _(b):
            block(g, old, new, weight, load, first + BLOCK * b, BLOCK, ks)

        if last - first > whole * BLOCK:
            at = first + whole * BLOCK
            block(g, old, new, weight, load, at, last - at, ks)

    def sweep(g, old, new, weight, load, wider):
        part(g, old, new, weight, load, g.row_halo - wider, g.row_halo + g.rows + wider, range(g.pieces))

    def near(g, outside, inside):
        low = range(g.column_halo - outside, g.column_halo + inside)
        high = range(g.column_halo + g.columns - inside, g.column_halo + g.columns + outside)
        return sorted({c % g.pieces for c in (*low, *high)})

    def edges(g, old, new, weight, load, outside, inside):
        top, end = g.row_halo, g.row_halo + g.rows
        every = range(g.pieces)
        block(g, old, new, weight, load, top - outside, outside + inside, every)
        block(g, old, new, weight, load, end - inside, outside + inside, every)
        part(g, old, new, weight, load, top + inside, end - inside, near(g, outside, inside))

    def inner(g, old, new, weight, load, inside):
        ks = sorted(set(range(g.pieces)) - set(near(g, 0, inside)))
        first, last = g.row_halo + inside, g.row_halo + g.rows - inside
        part(g, old, new, weight, load, first, last, ks)

    loads[2].wait()
    send_raw("u_first", lambda read: read(raw[2]))
    loads[0].wait()
    send_raw("w", lambda read: 0.8 / (4.0 + read(raw[0])))
    loads[1].wait()
    send_raw("f", lambda read: 0.8 / (4.0 + read(raw[0])) * read(raw[1]))

    @pl.loop(0, coarse.rows)
    def _(row):
        total = [0.0] * coarse.pieces
        for half in range(RATIO):
            at = RATIO * row + half
            for k in range(fine.pieces):
                g4 = 4.0 + raw[0][pl.ds(at * fine.width + k, SUB, stride=fine.pieces), :]
                put(w, fine, at + fine.row_halo, k, 0.8 / g4)
                put(iw, fine, at, k, 1.25 * g4)
                total[k // RATIO] = total[k // RATIO] + g4
        for k in range(coarse.pieces):
            mean = total[k] * (1.0 / RATIO) - (4.0 * RATIO - 4.0)
            put(cw, coarse, row + coarse.row_halo, k, 0.8 / mean)


    @pl.loop(0, fine.rows, unroll=2)
    def _(row):
        for k in range(fine.pieces):
            put(u, fine, row + fine.row_halo, k, raw[2][pl.ds(row * fine.width + k, SUB, stride=fine.pieces), :])


    @pl.loop(0, fine.rows, unroll=2)
    def _(row):
        for k in range(fine.pieces):
            at = row + fine.row_halo
            put(f, fine, at, k, piece(w, fine, at, k) * raw[1][pl.ds(row * fine.width + k, SUB, stride=fine.pieces), :])

    sweep(fine, u, v, w, f, 0)
    receive("w", w)
    receive("u_first", u)
    receive("f", f)
    edges(fine, u, v, w, f, 1, 1)
    edges(fine, v, u, w, f, 0, 2)
    send("u_second", u)
    send("cw", cw)
    inner(fine, v, u, w, f, 2)
    sweep(fine, u, v, w, f, 0)
    receive("u_second", u)
    edges(fine, u, v, w, f, 1, 1)

    @pl.loop(0, coarse.rows)
    def _(row):
        total = [0.0] * coarse.pieces
        for half in range(RATIO):
            at = RATIO * row + half + fine.row_halo
            here, sums = around(v, fine, at)
            for k in range(fine.pieces):
                change = piece(f, fine, at, k) + piece(w, fine, at, k) * sums[k] - 0.8 * here[k]
                total[k // RATIO] = total[k // RATIO] + change * piece(
                    iw, fine, at - fine.row_halo, k
                )
        for k in range(coarse.pieces):
            at = row + coarse.row_halo
            put(cf, coarse, at, k, total[k] * (1.0 / RATIO) * piece(cw, coarse, at, k))

    send("cf", cf)
    receive("cw", cw)
    receive("cf", cf)
    old, new, spare = cf, ca, cb
    left = INNER - 1
    wider = 7
    while wider > 0:
        wider -= 1
        sweep(coarse, old, new, cw, cf, wider)
        old, new, spare = new, spare, new
        left -= 1
    send("cu", old)
    receive("cu", old)
    new = ca if old is cb else cb
    wider = 6
    while left > 0:
        wider -= 1
        sweep(coarse, old, new, cw, cf, wider)
        old, new = new, old
        left -= 1

    @pl.loop(-1, coarse.rows + 1)
    def _(row):
        for k in range(coarse.pieces):
            more = piece(old, coarse, row + coarse.row_halo, k)
            for half in range(RATIO):
                at = RATIO * row + half + fine.row_halo
                for part in range(RATIO):
                    put(v, fine, at, RATIO * k + part, piece(v, fine, at, RATIO * k + part) + more)

    edges(fine, v, u, w, f, 0, 2)
    send("u_third", u)
    inner(fine, v, u, w, f, 2)
    sweep(fine, u, v, w, f, 0)
    receive("u_third", u)
    edges(fine, u, v, w, f, 1, 1)
    chunk = fine.rows // CHUNKS
    for c in range(CHUNKS):
        first = fine.row_halo + c * chunk
        part(fine, v, out, w, f, first, first + chunk, range(fine.pieces))

        @pl.loop(c * chunk, (c + 1) * chunk, unroll=4)
        def _(row):
            at = pl.multiple_of(row * fine.width + fine.column_halo, SUB)
            out_hbm[row] = out[pl.ds(at, fine.columns), :]


def per_device(source_terms, initial_values, absorption):
    rows, columns, cases = source_terms.shape
    fine = Grid(rows, columns, ROWS, RATIO * HALO)
    coarse = Grid(rows // RATIO, columns // RATIO, HALO, HALO)
    grids = {"fine": fine, "coarse": coarse}

    def held(*shape):
        return pltpu.VMEM(shape + (cases,), jnp.float32)

    shapes = [held(rows * fine.width) for _ in range(3)]
    shapes += [held(fine.stored) for _ in range(4)]
    shapes += [held(rows * fine.width), held(rows * fine.width)]
    shapes += [held(coarse.stored) for _ in range(4)]
    count = len(TRADES) * len(DIRS)
    shapes += [
        pltpu.SemaphoreType.DMA((3,)),
        pltpu.SemaphoreType.DMA((CHUNKS,)),
        pltpu.SemaphoreType.DMA((count,)),
        pltpu.SemaphoreType.DMA((count,)),
    ]
    for name, which, depth in TRADES:
        g = grids[which]
        shapes += [
            held(2, depth, g.width),
            held(2, depth, g.rows),
            held(2, depth, g.width),
            held(2, depth, g.rows),
            held(4, depth, SUB),
        ]
    return pl.pallas_call(
        functools.partial(kernel, grids),
        out_shape=jax.ShapeDtypeStruct(source_terms.shape, jnp.float32),
        in_specs=[pl.BlockSpec(memory_space=pltpu.HBM)] * 3,
        out_specs=pl.BlockSpec(memory_space=pltpu.VMEM),
        scratch_shapes=shapes,
        compiler_params=pltpu.CompilerParams(
            collective_id=0, has_side_effects=True, vmem_limit_bytes=44 * 1024 * 1024
        ),
    )(*[pltpu.with_memory_space_constraint(x, pltpu.HBM) for x in (source_terms, initial_values, absorption)])


def solution(mesh):
    placed = P(("shift", "band"), "lane", None)
    return jax.shard_map(
        per_device,
        mesh=mesh,
        in_specs=(placed, placed, placed),
        out_specs=placed,
        check_vma=False,
    )
```

profile of v0, /device:TPU:30, one launch (start us, length us, event | category | flops | bytes accessed | tf_op | source)
XLA Modules:
  0.0 72.7 jit_solution(13047072685659243763)
XLA Ops:
  0.0 71.3 %shard_map.37 = f32[64,64,128]{2,1,0:T(8,128)S(1)} custom-call(f32[64,64,128]{2,1,0:T(8,128)} %src_hbm.1, f32[64,64,128]{2,1,0:T(8,128)} %init_hbm.1, f32[64,64,128]{2,1,0:T(8,128)} %abs_hbm.1), custom_call_target="tpu_custom_call" | custom-call | tf_op jit(solution)/shard_map/pallas_call | solution.py:417
  71.3 1.3 %copy.5 = f32[64,64,128]{2,1,0:T(8,128)} copy(f32[64,64,128]{2,1,0:T(8,128)S(1)} %shard_map.37) | data formatting | bytes 4194304
where the time goes:
time: 74 us; the launch traced here: 72.7 us
  Pallas kernels  71.3 us (96%)
  local copies, waits for them, and re-layouts  1.32 us (2%)
    pallas_call x1, Pallas kernels, per_device(): pl.pallas_call(functools.partial(kernel, grids), out_shape=jax.ShapeDtype...  71.3 us

commit v1 on v0

v1 whole, which is shorter than its diff:
```python
import functools

import jax
import jax.numpy as jnp
from jax import lax
from jax.experimental import pallas as pl
from jax.experimental.pallas import tpu as pltpu
from jax.sharding import PartitionSpec as P

RATIO = 2
INNER = 13
SUB = 8
BLOCK = 4
MESH = pl.DeviceIdType.MESH
DIRS = [(-1, 0), (1, 0), (0, -1), (0, 1), (-1, -1), (-1, 1), (1, -1), (1, 1)]
TOP = 4
CTOP = 16
LEVELS = 14
PITCH = 88
MARGIN = 8


class Grid:
    def __init__(self, columns, pieces, halo):
        self.columns, self.pieces, self.halo = columns, pieces, halo
        self.width = pieces * SUB
        self.stored = columns + 2 * halo

    def at(self, column, piece=0):
        return pl.multiple_of((column + self.halo) * self.width + piece * SUB, SUB)

    def boxes(self, ref):
        return ref.reshape(self.stored, self.pieces, SUB, 128)


def kernel(fine, coarse, src_hbm, init_hbm, abs_hbm, out_ref, *scratch):
    u, v, x, w, f, y, iw, ra, rs, cw, cf, ca, cb, out, sums, in_sem, send_sem, recv_sem = scratch
    band, lane = lax.axis_index("band"), lax.axis_index("lane")
    bands, lanes = lax.axis_size("band"), lax.axis_size("lane")
    rows = fine.columns
    right = lane < lanes // 2

    def exists(q):
        dy, dx = q
        there = None
        if dy:
            there = (band > 0) if dy < 0 else (band < bands - 1)
        if dx:
            beside = (lane > 0) if dx < 0 else (lane < lanes - 1)
            there = beside if not dy else there & beside
        return there

    def name_of(q):
        return {"band": band + q[0], "lane": lane + q[1]}

    def late(q):
        return right if q[1] > 0 else jnp.logical_not(right)

    def side(if_right, if_left):
        return jnp.where(right, if_right, if_left)

    barrier = pltpu.get_barrier_semaphore()
    for q in DIRS:
        @pl.when(exists(q))
        def _():
            pl.semaphore_signal(barrier, inc=1, device_id=name_of(q), device_id_type=MESH)

    inputs = ((abs_hbm, ra), (src_hbm, rs), (init_hbm, u))
    for i, (ref, held) in enumerate(inputs):
        @pl.loop(0, rows)
        def _(row):
            at = row + TOP
            place = (at % fine.pieces) * SUB + at // fine.pieces
            to = held.reshape(fine.stored, fine.width, 128).at[
                pl.ds(fine.halo, fine.columns), pl.ds(place, 1), :
            ]
            pltpu.make_async_copy(ref.at[row].reshape(fine.columns, 1, 128), to, in_sem.at[i]).start()

    def loaded(i):
        ref, held = inputs[i]
        whole = held.reshape(fine.stored, fine.width, 128).at[pl.ds(fine.halo, fine.columns), pl.ds(0, rows), :]
        pltpu.make_async_copy(ref, whole, in_sem.at[i]).wait()

    zero = jnp.zeros((SUB, 128), jnp.float32)
    for dx in (-1, 1):
        @pl.when(jnp.logical_not(exists((0, dx))))
        def _():
            for g, refs, depth in ((fine, (u, w, f, y), 4), (coarse, (cw, cf), LEVELS)):
                @pl.loop(0, depth)
                def _(j):
                    column = j - depth if dx < 0 else g.columns + j
                    for ref in refs:
                        for p in range(g.pieces):
                            ref[pl.ds(g.at(column, p), SUB), :] = zero

    for dy in (-1, 1):
        @pl.when(jnp.logical_not(exists((dy, 0))))
        def _():
            @pl.loop(0, fine.stored // SUB)
            def _(j):
                for ref in (u, w, f, y):
                    for p in range(TOP):
                        place = p * SUB if dy < 0 else (fine.pieces - 1 - p) * SUB + SUB - 1
                        ref[pl.ds(j * SUB * fine.width + place, SUB, stride=fine.width), :] = zero

            @pl.loop(0, coarse.stored)
            def _(j):
                for ref in (cw, cf):
                    for p in range(coarse.pieces):
                        at = coarse.width * j + p * SUB + (0 if dy < 0 else SUB - 2)
                        ref[pl.ds(at, 2), :] = zero[:2]

    def columns_of(g, dx, depth, skip=0):
        if dx > 0:
            return g.halo + g.columns - depth - skip, g.halo - depth - skip, depth
        return g.halo + skip, g.halo + g.columns + skip, depth

    def fine_rows(dy, depth):
        if dy > 0:
            return (5 - depth, 7), (4 - depth, 0), (depth, 1)
        return (4, 0), (5, 7), (depth, 1)

    def coarse_rows(dy, depth):
        d = depth // SUB
        if dy > 0:
            return (0, 6 - d), (0, 2 - d), (SUB, d)
        return (0, 2), (0, 6), (SUB, d)

    own = [((0, 1), (0, 1), (4, 7)), ((4, 0), (4, 0), (1, 8)), ((5, 0), (5, 0), (4, 7))]
    middle = [((0, 2), (0, 2), (SUB, 4))]

    copies = {}
    counter = [0]

    def add(name, g, source, target, q, columns, places):
        from_column, to_column, count = columns
        for (p, s), (pt, st), (np_, ns) in places:
            here = g.boxes(source).at[pl.ds(from_column, count), pl.ds(p, np_), pl.ds(s, ns), :]
            there = g.boxes(target).at[pl.ds(to_column, count), pl.ds(pt, np_), pl.ds(st, ns), :]
            copies.setdefault((name, q), []).append((here, there))

    def fine_set(name, source, target, depth, corner):
        for q in DIRS:
            dy, dx = q
            if not dy:
                add(name, fine, source, target, q, columns_of(fine, dx, depth), own)
            elif not dx:
                add(name, fine, source, target, q, (fine.halo, fine.halo, fine.columns), [fine_rows(dy, depth)])
            else:
                add(name, fine, source, target, q, columns_of(fine, dx, corner), [fine_rows(dy, corner)])

    fine_set("u", u, u, 4, 3)
    fine_set("w", w, w, 3, 2)
    fine_set("f", f, f, 3, 2)
    fine_set("y", v, y, 3, 2)
    for q in DIRS:
        dy, dx = q
        if not dy:
            add("cw", coarse, cw, cw, q, columns_of(coarse, dx, LEVELS - 1), middle)
            add("near", coarse, cf, cf, q, columns_of(coarse, dx, 2), middle)
            add("far", coarse, cf, cf, q, columns_of(coarse, dx, LEVELS - 2, 2), middle)
        elif not dx:
            place = [coarse_rows(dy, 16)]
            add("cw", coarse, cw, cw, q, (coarse.halo, coarse.halo, coarse.columns), place)
            at = coarse.halo + side(coarse.columns - 2, 0)
            add("near", coarse, cf, cf, q, (at, at, 2), place)
            at = coarse.halo + side(0, 2)
            add("far", coarse, cf, cf, q, (at, at, coarse.columns - 2), place)
        else:
            add("cw", coarse, cw, cw, q, columns_of(coarse, dx, 5), [coarse_rows(dy, 16)])
            add("cw", coarse, cw, cw, q, columns_of(coarse, dx, 7, 5), [coarse_rows(dy, 8)])
            add("near", coarse, cf, cf, q, columns_of(coarse, dx, 2), [coarse_rows(dy, 16)])
            add("far", coarse, cf, cf, q, columns_of(coarse, dx, 3, 2), [coarse_rows(dy, 16)])
            add("far", coarse, cf, cf, q, columns_of(coarse, dx, 8, 5), [coarse_rows(dy, 8)])

    first = {}
    for key in sorted(copies, key=lambda k: (k[0], DIRS.index(k[1]))):
        first[key] = counter[0]
        counter[0] += len(copies[key])

    def copies_of(name, q, arriving):
        back = (-q[0], -q[1])
        sent = copies[name, back if arriving else q]
        for i, (here, there) in enumerate(sent):
            yield pltpu.make_async_remote_copy(
                src_ref=here,
                dst_ref=there,
                send_sem=send_sem.at[first[name, q] + i],
                recv_sem=recv_sem.at[first[name, q if arriving else back] + i],
                device_id=name_of(q),
                device_id_type=MESH,
            )

    def start(name, q, when=None):
        @pl.when(exists(q) if when is None else exists(q) & when)
        def _():
            for copy in copies_of(name, q, False):
                copy.start()

    def sent(names):
        for name in names:
            for q in DIRS:
                @pl.when(exists(q))
                def _():
                    for copy in copies_of(name, q, False):
                        copy.wait_send()

    def arrived(names, q, when=None):
        @pl.when(exists(q) if when is None else exists(q) & when)
        def _():
            for name in names:
                for copy in copies_of(name, q, True):
                    copy.wait_recv()

    rows_only, sides, corners = DIRS[:2], DIRS[2:4], DIRS[4:]

    def early_arrived(names):
        for q in rows_only:
            arrived(names, q)
        for q in sides + corners:
            arrived(names, q, jnp.logical_not(late(q)))

    def late_arrived(names):
        for q in sides + corners:
            arrived(names, q, late(q))

    def get(g, ref, column, p):
        return ref[pl.ds(g.at(column, p), SUB), :]

    def stencil(g, old, column, p, count):
        here = [get(g, old, column + j, p) for j in range(-1, count + 1)]
        found = []
        for j in range(count):
            up = get(g, old, column + j, p - 1) if p else pltpu.roll(get(g, old, column + j, g.pieces - 1), 1, 0)
            if p < g.pieces - 1:
                down = get(g, old, column + j, p + 1)
            else:
                down = pltpu.roll(get(g, old, column + j, 0), SUB - 1, 0)
            found.append((here[j + 1], (up + down) + (here[j] + here[j + 2])))
        return found

    def sweep(g, old, new, weight, load, at, blocks):
        @pl.loop(0, blocks)
        def _(b):
            column = at + BLOCK * b
            for p in range(g.pieces):
                for j, (here, total) in enumerate(stencil(g, old, column, p, BLOCK)):
                    c = column + j
                    value = 0.2 * here + get(g, load, c, p) + get(g, weight, c, p) * total
                    if new is out:
                        new[pl.ds(p * PITCH + c + MARGIN, SUB, stride=g.pieces * PITCH), :] = value
                    else:
                        new[pl.ds(g.at(c, p), SUB), :] = value

    def natural(ref, column, i):
        return ref[pl.ds((column + coarse.halo) * coarse.width + 2 + i, SUB, stride=coarse.pieces), :]

    def put_natural(ref, column, i, value):
        ref[pl.ds((column + coarse.halo) * coarse.width + 2 + i, SUB, stride=coarse.pieces), :] = value

    def paired(slot, i):
        at = slot * 96 + 16 * i + TOP
        return sums[pl.ds(at, SUB, stride=2), :] + sums[pl.ds(at + 1, SUB, stride=2), :]

    def restrict(at, blocks):
        @pl.loop(0, blocks)
        def _(b):
            column = at + RATIO * b
            for p in range(fine.pieces):
                found = stencil(fine, v, RATIO * column, p, BLOCK)
                defects = []
                for j, (here, total) in enumerate(found):
                    c = RATIO * column + j
                    change = get(fine, f, c, p) + get(fine, w, c, p) * total - 0.8 * here
                    defects.append(change * get(fine, iw, c, p))
                for slot in range(2):
                    sums[pl.ds(slot * 96 + p, SUB, stride=fine.pieces), :] = defects[2 * slot] + defects[2 * slot + 1]
            for slot in range(2):
                for i in range(4):
                    put_natural(
                        cf, column + slot, i, (paired(slot, i) * (1.0 / RATIO)) * natural(cw, column + slot, i)
                    )

    def correct(values, at, blocks):
        @pl.loop(0, blocks)
        def _(b):
            column = at + RATIO * b
            for slot in range(2):
                for i in range(-1, 5):
                    more = natural(values, column + slot, i)
                    place = slot * 96 + 16 * (i + 1)
                    sums[pl.ds(place, SUB, stride=2), :] = more
                    sums[pl.ds(place + 1, SUB, stride=2), :] = more
            for slot in range(2):
                for p in range(fine.pieces):
                    more = sums[pl.ds(slot * 96 + CTOP - TOP + p, SUB, stride=fine.pieces), :]
                    for j in range(RATIO):
                        c = fine.at(RATIO * (column + slot) + j, p)
                        v[pl.ds(c, SUB), :] = v[pl.ds(c, SUB), :] + more

    loaded(0)
    loaded(1)

    @pl.loop(0, fine.columns)
    def _(c):
        for p in range(fine.pieces):
            s, n = (1, 7) if p < 4 else (0, 8) if p == 4 else (0, 7)
            at = (c + fine.halo) * fine.width + p * SUB + s
            g4 = 4.0 + ra[pl.ds(at, n), :]
            weight = 0.8 / g4
            w[pl.ds(at, n), :] = weight
            f[pl.ds(at, n), :] = weight * rs[pl.ds(at, n), :]
            iw[pl.ds(at, n), :] = 1.25 * g4

    @pl.loop(0, coarse.columns // 2)
    def _(b):
        for slot in range(2):
            c = RATIO * (2 * b + slot)
            for p in range(fine.pieces):
                total = (4.0 + get(fine, ra, c, p)) + (4.0 + get(fine, ra, c + 1, p))
                sums[pl.ds(slot * 96 + p, SUB, stride=fine.pieces), :] = total
        for slot in range(2):
            for i in range(4):
                mean = paired(slot, i) * (1.0 / RATIO) - (4.0 * RATIO - 4.0)
                put_natural(cw, 2 * b + slot, i, 0.8 / mean)

    loaded(2)
    on_band = (band > 0).astype(jnp.int32) + (band < bands - 1).astype(jnp.int32)
    on_lane = (lane > 0).astype(jnp.int32) + (lane < lanes - 1).astype(jnp.int32)
    pl.semaphore_wait(barrier, (on_band + 1) * (on_lane + 1) - 1)

    for name in ("u", "w", "f"):
        for q in sides:
            start(name, q)
    for name in ("u", "w", "f"):
        for q in corners:
            start(name, q)
    for name in ("u", "w", "f"):
        for q in rows_only:
            start(name, q)
    for q in sides + corners + rows_only:
        start("cw", q)

    before = ((u, v), (v, x), (x, v))
    early_arrived(("u", "w", "f"))
    for k, (old, new) in enumerate(before, 1):
        width = 4 * -(-(68 - 2 * k) // 4)
        sweep(fine, old, new, w, f, side(64 - k - width, k), width // 4)
    restrict(side(0, 2), 15)
    for q in sides + corners:
        start("far", q)
    for q in sides + corners:
        start("near", q, jnp.logical_not(late(q)))
    for q in rows_only:
        start("far", q)
    late_arrived(("u", "w", "f"))
    for k, (old, new) in enumerate(before, 1):
        sweep(fine, old, new, w, f, side(64 - k, k - 4), 1)
    restrict(side(30, 0), 1)
    for q in sides + corners:
        start("near", q, late(q))
    for q in rows_only:
        start("near", q)
    for q in sides + corners + rows_only:
        start("y", q)

    inner = []
    old = cf
    for k in range(2, INNER + 1):
        new = ca if k % 2 == 0 else cb
        inner.append((k, old, new))
        old = new
    sent(("u", "w", "f", "cw"))
    early_arrived(("cw", "far", "near"))
    for k, old, new in inner:
        width = 4 * -(-(48 - 2 * k) // 4)
        sweep(coarse, old, new, cw, cf, side(33 - k - width, k - 1), width // 4)

    last = inner[-1][2]
    after = ((v, u), (u, v), (v, out))

    def take(column):
        @pl.loop(0, 3)
        def _(j):
            for p in range(fine.pieces):
                at = fine.at(column + j, p)
                v[pl.ds(at, SUB), :] = y[pl.ds(at, SUB), :]

    def deliver(at):
        @pl.loop(0, rows)
        def _(row):
            for i in range(4):
                c = pl.multiple_of(at + SUB * i, SUB)
                place = pl.multiple_of((row + TOP) * PITCH + MARGIN + c, SUB)
                out_ref[row, pl.ds(c, SUB), :] = out[pl.ds(place, SUB), :]

    sent(("y", "far", "near"))
    early_arrived(("y",))

    @pl.loop(0, fine.columns // SUB)
    def _(j):
        for p, s in ((1, 0), (2, 0), (3, 0), (5, 7), (6, 7), (7, 7)):
            at = (j * SUB + fine.halo) * fine.width + p * SUB + s
            v[pl.ds(at, SUB, stride=fine.width), :] = y[pl.ds(at, SUB, stride=fine.width), :]

    take(side(-3, 64))
    correct(last, side(-2, 12), 11)
    for m, (old, new) in enumerate(after, 1):
        width = 4 * -(-(43 - 2 * m) // 4)
        sweep(fine, old, new, w, f, side(40 - m - width, 24 + m), width // 4)
    deliver(side(0, 32))

    late_arrived(("cw", "far", "near"))
    for k, old, new in inner:
        sweep(coarse, old, new, cw, cf, side(33 - k, k - 17), 4)
    late_arrived(("y",))
    take(side(64, -3))
    correct(last, side(20, -2), 7)
    for m, (old, new) in enumerate(after, 1):
        sweep(fine, old, new, w, f, side(40 - m, m - 4), 7)
    deliver(side(32, 0))


def per_device(source_terms, initial_values, absorption):
    rows, columns, cases = source_terms.shape
    fine = Grid(columns, (rows + 2 * TOP) // SUB, 8)
    coarse = Grid(columns // RATIO, (rows // RATIO + 2 * CTOP) // SUB, 18)

    def held(*shape):
        return pltpu.VMEM(shape + (cases,), jnp.float32)

    shapes = [held(fine.stored * fine.width) for _ in range(9)]
    shapes += [held(coarse.stored * coarse.width) for _ in range(4)]
    shapes += [held((rows + 2 * TOP) * PITCH), held(2 * 96)]
    count = 128
    shapes += [
        pltpu.SemaphoreType.DMA((3,)),
        pltpu.SemaphoreType.DMA((count,)),
        pltpu.SemaphoreType.DMA((count,)),
    ]
    return pl.pallas_call(
        functools.partial(kernel, fine, coarse),
        out_shape=jax.ShapeDtypeStruct(source_terms.shape, jnp.float32),
        in_specs=[pl.BlockSpec(memory_space=pltpu.HBM)] * 3,
        out_specs=pl.BlockSpec(memory_space=pltpu.VMEM),
        scratch_shapes=shapes,
        compiler_params=pltpu.CompilerParams(
            collective_id=0, has_side_effects=True, vmem_limit_bytes=52 * 1024 * 1024
        ),
    )(*[pltpu.with_memory_space_constraint(x, pltpu.HBM) for x in (source_terms, initial_values, absorption)])


def solution(mesh):
    placed = P(("shift", "band"), "lane", None)
    return jax.shard_map(
        per_device,
        mesh=mesh,
        in_specs=(placed, placed, placed),
        out_specs=placed,
        check_vma=False,
    )
```

time: 74 us -> 92.1 us (1.24); the launches traced: 72.7 us -> 91.9 us
  Pallas kernels: 71.3 us -> 88.8 us
  local copies, waits for them, and re-layouts: 1.32 us -> 3.16 us
    pallas_call x1, Pallas kernels: 71.3 us -> 88.8 us  [per_device(): pl.pallas_call(functools.partial(kernel, fine, coarse), out_shape=jax.Sha...]
    unnamed x1, local copies, waits for them, and re-layouts: 1.32 us -> 3.16 us
where the time goes in v1:
time: 92.1 us; the launch traced here: 91.9 us
  Pallas kernels  88.8 us (96%)
  local copies, waits for them, and re-layouts  3.16 us (3%)
    pallas_call x1, Pallas kernels, per_device(): pl.pallas_call(functools.partial(kernel, fine, coarse), out_shape=jax.Sha...  88.8 us
    unnamed x1, local copies, waits for them, and re-layouts  3.16 us

profile of v1, /device:TPU:30, one launch (start us, length us, event | category | flops | bytes accessed | tf_op | source)
XLA Modules:
  0.0 91.9 jit_solution(16872319545135170906)
XLA Ops:
  0.0 88.8 %shard_map.37 = f32[64,64,128]{2,1,0:T(8,128)} custom-call(f32[64,64,128]{2,1,0:T(8,128)} %src_hbm.1, f32[64,64,128]{2,1,0:T(8,128)} %init_hbm.1, f32[64,64,128]{2,1,0:T(8,128)} %abs_hbm.1), custom_call_target="tpu_custom_call" | custom-call | tf_op jit(solution)/shard_map/pallas_call | solution.py:441
  88.8 3.2 %copy.5 = f32[64,64,128]{2,1,0:T(8,128)} copy(f32[64,64,128]{2,1,0:T(8,128)} %shard_map.37) | data formatting | bytes 4194304

commit v2 on v1

--- a/solution.py
+++ b/solution.py
@@ -34,7 +34,7 @@
 
 
 def kernel(fine, coarse, src_hbm, init_hbm, abs_hbm, out_ref, *scratch):
-    u, v, x, w, f, y, iw, ra, rs, cw, cf, ca, cb, out, sums, in_sem, send_sem, recv_sem = scratch
+    u, v, x, w, f, y, iw, ra, rs, cw, cf, ca, cb, out, sums, fine_relay, coarse_relay, in_sem, send_sem, recv_sem, pass_sem, land_sem = scratch
     band, lane = lax.axis_index("band"), lax.axis_index("lane")
     bands, lanes = lax.axis_size("band"), lax.axis_size("lane")
     rows = fine.columns
@@ -59,11 +59,26 @@
     def side(if_right, if_left):
         return jnp.where(right, if_right, if_left)
 
+    low, high = lanes // 2 - 1, lanes // 2
+    ends = {(0, 1): (low, high), (0, -1): (high, low)}
+    relays = {
+        (0, 1): {1: lanes // 4 - 1, 2: 0},
+        (0, -1): {1: lanes - lanes // 4, 2: lanes - 1},
+    }
+    legs = []
+    for q, (source, target) in ends.items():
+        for relay in relays[q].values():
+            legs += [(source, relay), (relay, source), (relay, target), (target, relay)]
+
     barrier = pltpu.get_barrier_semaphore()
     for q in DIRS:
         @pl.when(exists(q))
         def _():
             pl.semaphore_signal(barrier, inc=1, device_id=name_of(q), device_id_type=MESH)
+    for source, target in legs:
+        @pl.when(lane == source)
+        def _():
+            pl.semaphore_signal(barrier, inc=1, device_id={"lane": target}, device_id_type=MESH)
 
     inputs = ((abs_hbm, ra), (src_hbm, rs), (init_hbm, u))
     for i, (ref, held) in enumerate(inputs):
@@ -121,57 +136,75 @@
         return (4, 0), (5, 7), (depth, 1)
 
     def coarse_rows(dy, depth):
-        d = depth // SUB
+        e = depth - SUB
+        if e <= 0:
+            if dy > 0:
+                return [((SUB - depth, 5), (SUB - depth, 1), (depth, 1))]
+            return [((0, 2), (0, 6), (depth, 1))]
         if dy > 0:
-            return (0, 6 - d), (0, 2 - d), (SUB, d)
-        return (0, 2), (0, 6), (SUB, d)
+            return [((SUB - e, 4), (SUB - e, 0), (e, 2)), ((0, 5), (0, 1), (SUB - e, 1))]
+        return [((0, 2), (0, 6), (e, 2)), ((e, 2), (e, 6), (SUB - e, 1))]
 
     own = [((0, 1), (0, 1), (4, 7)), ((4, 0), (4, 0), (1, 8)), ((5, 0), (5, 0), (4, 7))]
     middle = [((0, 2), (0, 2), (SUB, 4))]
 
-    copies = {}
+    copies, used = {}, {}
+    offsets = {"w": 0, "f": 0, "y": 9, "cw": 0, "far": 4}
     counter = [0]
 
-    def add(name, g, source, target, q, columns, places):
+    def add(name, g, source, target, q, columns, places, paths=(0,)):
         from_column, to_column, count = columns
-        for (p, s), (pt, st), (np_, ns) in places:
+        for i, ((p, s), (pt, st), (np_, ns)) in enumerate(places):
             here = g.boxes(source).at[pl.ds(from_column, count), pl.ds(p, np_), pl.ds(s, ns), :]
             there = g.boxes(target).at[pl.ds(to_column, count), pl.ds(pt, np_), pl.ds(st, ns), :]
-            copies.setdefault((name, q), []).append((here, there))
-
-    def fine_set(name, source, target, depth, corner):
+            path = paths[i % len(paths)]
+            relay = None
+            if path:
+                held = fine_relay if g is fine else coarse_relay
+                base = used.setdefault((name, q, path), 0)
+                used[name, q, path] = base + count
+                base += offsets[name]
+                relay = held.reshape(held.shape[0] // g.width, g.pieces, SUB, 128).at[
+                    pl.ds(base, count), pl.ds(p, np_), pl.ds(s, ns), :
+                ]
+            copies.setdefault((name, q), []).append((here, there, path, relay))
+
+    def fine_set(name, source, target, depth, corner, paths=(0,)):
         for q in DIRS:
             dy, dx = q
             if not dy:
-                add(name, fine, source, target, q, columns_of(fine, dx, depth), own)
+                add(name, fine, source, target, q, columns_of(fine, dx, depth), own, paths)
             elif not dx:
                 add(name, fine, source, target, q, (fine.halo, fine.halo, fine.columns), [fine_rows(dy, depth)])
             else:
                 add(name, fine, source, target, q, columns_of(fine, dx, corner), [fine_rows(dy, corner)])
 
     fine_set("u", u, u, 4, 3)
-    fine_set("w", w, w, 3, 2)
-    fine_set("f", f, f, 3, 2)
-    fine_set("y", v, y, 3, 2)
+    fine_set("w", w, w, 3, 2, (1,))
+    fine_set("f", f, f, 3, 2, (2,))
+    fine_set("y", v, y, 3, 2, (1, 0, 2))
     for q in DIRS:
         dy, dx = q
         if not dy:
-            add("cw", coarse, cw, cw, q, columns_of(coarse, dx, LEVELS - 1), middle)
             add("near", coarse, cf, cf, q, columns_of(coarse, dx, 2), middle)
-            add("far", coarse, cf, cf, q, columns_of(coarse, dx, LEVELS - 2, 2), middle)
+            for path, (count, skip) in enumerate(((5, 0), (4, 5), (4, 9))):
+                add("cw", coarse, cw, cw, q, columns_of(coarse, dx, count, skip), middle, (path,))
+            for path, skip in enumerate((2, 6, 10)):
+                add("far", coarse, cf, cf, q, columns_of(coarse, dx, 4, skip), middle, (path,))
         elif not dx:
-            place = [coarse_rows(dy, 16)]
+            place = coarse_rows(dy, LEVELS - 1)
             add("cw", coarse, cw, cw, q, (coarse.halo, coarse.halo, coarse.columns), place)
+            place = coarse_rows(dy, LEVELS)
             at = coarse.halo + side(coarse.columns - 2, 0)
             add("near", coarse, cf, cf, q, (at, at, 2), place)
             at = coarse.halo + side(0, 2)
             add("far", coarse, cf, cf, q, (at, at, coarse.columns - 2), place)
         else:
-            add("cw", coarse, cw, cw, q, columns_of(coarse, dx, 5), [coarse_rows(dy, 16)])
-            add("cw", coarse, cw, cw, q, columns_of(coarse, dx, 7, 5), [coarse_rows(dy, 8)])
-            add("near", coarse, cf, cf, q, columns_of(coarse, dx, 2), [coarse_rows(dy, 16)])
-            add("far", coarse, cf, cf, q, columns_of(coarse, dx, 3, 2), [coarse_rows(dy, 16)])
-            add("far", coarse, cf, cf, q, columns_of(coarse, dx, 8, 5), [coarse_rows(dy, 8)])
+            for count, skip, depth in ((2, 0, 12), (3, 2, 10), (4, 5, 7), (3, 9, 3)):
+                add("cw", coarse, cw, cw, q, columns_of(coarse, dx, count, skip), coarse_rows(dy, depth))
+            for count, skip, depth in ((2, 0, 13), (3, 2, 11), (4, 5, 8), (4, 9, 4)):
+                name = "far" if skip else "near"
+                add(name, coarse, cf, cf, q, columns_of(coarse, dx, count, skip), coarse_rows(dy, depth))
 
     first = {}
     for key in sorted(copies, key=lambda k: (k[0], DIRS.index(k[1]))):
@@ -180,9 +213,8 @@
 
     def copies_of(name, q, arriving):
         back = (-q[0], -q[1])
-        sent = copies[name, back if arriving else q]
-        for i, (here, there) in enumerate(sent):
-            yield pltpu.make_async_remote_copy(
+        for i, (here, there, path, relay) in enumerate(copies[name, back if arriving else q]):
+            yield path, pltpu.make_async_remote_copy(
                 src_ref=here,
                 dst_ref=there,
                 send_sem=send_sem.at[first[name, q] + i],
@@ -191,25 +223,71 @@
                 device_id_type=MESH,
             )
 
+    def legs_of(name, q):
+        back = (-q[0], -q[1])
+        for i, (here, there, path, relay) in enumerate(copies[name, q]):
+            if path:
+                yield path, pltpu.make_async_remote_copy(
+                    src_ref=here,
+                    dst_ref=relay,
+                    send_sem=send_sem.at[first[name, q] + i],
+                    recv_sem=land_sem.at[first[name, q] + i],
+                    device_id={"lane": relays[q][path]},
+                    device_id_type=MESH,
+                ), pltpu.make_async_remote_copy(
+                    src_ref=relay,
+                    dst_ref=there,
+                    send_sem=pass_sem.at[first[name, q] + i],
+                    recv_sem=recv_sem.at[first[name, back] + i],
+                    device_id={"lane": ends[q][1]},
+                    device_id_type=MESH,
+                )
+
     def start(name, q, when=None):
-        @pl.when(exists(q) if when is None else exists(q) & when)
+        ready = exists(q) if when is None else exists(q) & when
+        direct = ready
+        if any(path for *_, path, relay in copies[name, q]):
+            direct = ready & (lane != ends[q][0])
+
+            @pl.when(ready & (lane == ends[q][0]))
+            def _():
+                for path, copy in copies_of(name, q, False):
+                    if not path:
+                        copy.start()
+                for path, there, on in legs_of(name, q):
+                    there.start()
+
+        @pl.when(direct)
         def _():
-            for copy in copies_of(name, q, False):
+            for path, copy in copies_of(name, q, False):
                 copy.start()
+
+    def pass_on(names, finish=False):
+        for q in ends:
+            for way, relay_lane in relays[q].items():
+                @pl.when(lane == relay_lane)
+                def _():
+                    for name in names:
+                        for path, there, on in legs_of(name, q):
+                            if path == way and finish:
+                                on.wait_send()
+                            elif path == way:
+                                there.wait_recv()
+                                on.start()
 
     def sent(names):
         for name in names:
             for q in DIRS:
                 @pl.when(exists(q))
                 def _():
-                    for copy in copies_of(name, q, False):
+                    for path, copy in copies_of(name, q, False):
                         copy.wait_send()
 
     def arrived(names, q, when=None):
         @pl.when(exists(q) if when is None else exists(q) & when)
         def _():
             for name in names:
-                for copy in copies_of(name, q, True):
+                for path, copy in copies_of(name, q, True):
                     copy.wait_recv()
 
     rows_only, sides, corners = DIRS[:2], DIRS[2:4], DIRS[4:]
@@ -327,7 +405,8 @@
     loaded(2)
     on_band = (band > 0).astype(jnp.int32) + (band < bands - 1).astype(jnp.int32)
     on_lane = (lane > 0).astype(jnp.int32) + (lane < lanes - 1).astype(jnp.int32)
-    pl.semaphore_wait(barrier, (on_band + 1) * (on_lane + 1) - 1)
+    on_leg = sum((lane == source).astype(jnp.int32) for source, target in legs)
+    pl.semaphore_wait(barrier, (on_band + 1) * (on_lane + 1) - 1 + on_leg)
 
     for name in ("u", "w", "f"):
         for q in sides:
@@ -340,6 +419,7 @@
             start(name, q)
     for q in sides + corners + rows_only:
         start("cw", q)
+    pass_on(("w", "f"))
 
     before = ((u, v), (v, x), (x, v))
     early_arrived(("u", "w", "f"))
@@ -364,6 +444,8 @@
     for q in sides + corners + rows_only:
         start("y", q)
 
+    pass_on(("cw", "far", "y"))
+
     inner = []
     old = cf
     for k in range(2, INNER + 1):
@@ -395,6 +477,7 @@
                 out_ref[row, pl.ds(c, SUB), :] = out[pl.ds(place, SUB), :]
 
     sent(("y", "far", "near"))
+    pass_on(("w", "f", "cw", "far", "y"), finish=True)
     early_arrived(("y",))
 
     @pl.loop(0, fine.columns // SUB)
@@ -432,9 +515,12 @@
     shapes = [held(fine.stored * fine.width) for _ in range(9)]
     shapes += [held(coarse.stored * coarse.width) for _ in range(4)]
     shapes += [held((rows + 2 * TOP) * PITCH), held(2 * 96)]
-    count = 128
+    shapes += [held(12 * fine.width), held(8 * coarse.width)]
+    count = 144
     shapes += [
         pltpu.SemaphoreType.DMA((3,)),
+        pltpu.SemaphoreType.DMA((count,)),
+        pltpu.SemaphoreType.DMA((count,)),
         pltpu.SemaphoreType.DMA((count,)),
         pltpu.SemaphoreType.DMA((count,)),
     ]

time: 92.1 us -> 66.8 us (0.73)
  Pallas kernels: 88.8 us -> 63.4 us
    pallas_call x1, Pallas kernels: 88.8 us -> 63.4 us  [per_device(): pl.pallas_call(functools.partial(kernel, fine, coarse), out_shape=jax.Sha...]
where the time goes in v2:
time: 66.8 us; the launch traced here: 66.6 us
  Pallas kernels  63.4 us (95%)
  local copies, waits for them, and re-layouts  3.16 us (5%)
    pallas_call x1, Pallas kernels, per_device(): pl.pallas_call(functools.partial(kernel, fine, coarse), out_shape=jax.Sha...  63.4 us
    unnamed x1, local copies, waits for them, and re-layouts  3.16 us

profile of v2, /device:TPU:30, one launch (start us, length us, event | category | flops | bytes accessed | tf_op | source)
XLA Modules:
  0.0 66.6 jit_solution(3917707515904609359)
XLA Ops:
  0.0 63.4 %shard_map.37 = f32[64,64,128]{2,1,0:T(8,128)} custom-call(f32[64,64,128]{2,1,0:T(8,128)} %src_hbm.1, f32[64,64,128]{2,1,0:T(8,128)} %init_hbm.1, f32[64,64,128]{2,1,0:T(8,128)} %abs_hbm.1), custom_call_target="tpu_custom_call" | custom-call | tf_op jit(solution)/shard_map/pallas_call | solution.py:527
  63.4 3.2 %copy.5 = f32[64,64,128]{2,1,0:T(8,128)} copy(f32[64,64,128]{2,1,0:T(8,128)} %shard_map.37) | data formatting | bytes 4194304

commit v3 on v2

--- a/solution.py
+++ b/solution.py
@@ -33,8 +33,16 @@
         return ref.reshape(self.stored, self.pieces, SUB, 128)
 
 
-def kernel(fine, coarse, src_hbm, init_hbm, abs_hbm, out_ref, *scratch):
-    u, v, x, w, f, y, iw, ra, rs, cw, cf, ca, cb, out, sums, fine_relay, coarse_relay, in_sem, send_sem, recv_sem, pass_sem, land_sem = scratch
+def deliver(held, out_hbm, sem):
+    rows, columns, _ = out_hbm.shape
+    whole = held.reshape(rows + 2 * TOP, PITCH, 128).at[pl.ds(TOP, rows), pl.ds(MARGIN, columns), :]
+    copy = pltpu.make_async_copy(whole, out_hbm, sem)
+    copy.start()
+    copy.wait()
+
+
+def kernel(fine, coarse, src_hbm, init_hbm, abs_hbm, out, *scratch):
+    u, v, x, w, f, y, iw, ra, rs, cw, cf, ca, cb, sums, fine_relay, coarse_relay, in_sem, send_sem, recv_sem, pass_sem, land_sem = scratch
     band, lane = lax.axis_index("band"), lax.axis_index("lane")
     bands, lanes = lax.axis_size("band"), lax.axis_size("lane")
     rows = fine.columns
@@ -62,8 +70,8 @@
     low, high = lanes // 2 - 1, lanes // 2
     ends = {(0, 1): (low, high), (0, -1): (high, low)}
     relays = {
-        (0, 1): {1: lanes // 4 - 1, 2: 0},
-        (0, -1): {1: lanes - lanes // 4, 2: lanes - 1},
+        (0, 1): {1: lanes // 4 - 1, 2: 0, 3: lanes // 4},
+        (0, -1): {1: lanes - lanes // 4, 2: lanes - 1, 3: lanes - lanes // 4 - 1},
     }
     legs = []
     for q, (source, target) in ends.items():
@@ -130,10 +138,10 @@
             return g.halo + g.columns - depth - skip, g.halo - depth - skip, depth
         return g.halo + skip, g.halo + g.columns + skip, depth
 
-    def fine_rows(dy, depth):
+    def fine_rows(dy, depth, skip=0):
         if dy > 0:
-            return (5 - depth, 7), (4 - depth, 0), (depth, 1)
-        return (4, 0), (5, 7), (depth, 1)
+            return [((5 - depth - skip, 7), (4 - depth - skip, 0), (depth, 1))]
+        return [((4 + skip, 0), (5 + skip, 7), (depth, 1))]
 
     def coarse_rows(dy, depth):
         e = depth - SUB
@@ -148,9 +156,8 @@
     own = [((0, 1), (0, 1), (4, 7)), ((4, 0), (4, 0), (1, 8)), ((5, 0), (5, 0), (4, 7))]
     middle = [((0, 2), (0, 2), (SUB, 4))]
 
-    copies, used = {}, {}
-    offsets = {"w": 0, "f": 0, "y": 9, "cw": 0, "far": 4}
-    counter = [0]
+    copies, used, volume = {}, {}, {}
+    offsets = {"w": 0, "f": 3, "y": 9, "cw": 0, "far": 3}
 
     def add(name, g, source, target, q, columns, places, paths=(0,)):
         from_column, to_column, count = columns
@@ -168,29 +175,36 @@
                     pl.ds(base, count), pl.ds(p, np_), pl.ds(s, ns), :
                 ]
             copies.setdefault((name, q), []).append((here, there, path, relay))
-
-    def fine_set(name, source, target, depth, corner, paths=(0,)):
-        for q in DIRS:
-            dy, dx = q
-            if not dy:
-                add(name, fine, source, target, q, columns_of(fine, dx, depth), own, paths)
+            volume[name, q, path] = volume.get((name, q, path), 0) + count * np_ * ns
+
+    for q in DIRS:
+        dy, dx = q
+        for name, source, target, depth, corner in (("u", u, u, 4, 3), ("w", w, w, 3, 2), ("f", f, f, 3, 2)):
+            if not dy and name == "u":
+                add(name, fine, source, target, q, columns_of(fine, dx, depth), own)
+            elif not dy:
+                path = 1 if name == "w" else 2
+                add(name, fine, source, target, q, columns_of(fine, dx, 2), own, (path,))
+                add(name, fine, source, target, q, columns_of(fine, dx, 1, 2), own, (3,))
             elif not dx:
-                add(name, fine, source, target, q, (fine.halo, fine.halo, fine.columns), [fine_rows(dy, depth)])
+                add(name, fine, source, target, q, (fine.halo, fine.halo, fine.columns), fine_rows(dy, depth))
             else:
-                add(name, fine, source, target, q, columns_of(fine, dx, corner), [fine_rows(dy, corner)])
-
-    fine_set("u", u, u, 4, 3)
-    fine_set("w", w, w, 3, 2, (1,))
-    fine_set("f", f, f, 3, 2, (2,))
-    fine_set("y", v, y, 3, 2, (1, 0, 2))
+                add(name, fine, source, target, q, columns_of(fine, dx, corner), fine_rows(dy, corner))
+        if not dy:
+            add("y", fine, v, y, q, columns_of(fine, dx, 2, 1), own, (1, 0, 3))
+        elif not dx:
+            add("y", fine, v, y, q, (fine.halo, fine.halo, fine.columns), fine_rows(dy, 2, 1))
+        else:
+            add("y", fine, v, y, q, columns_of(fine, dx, 2), fine_rows(dy, 2))
+
     for q in DIRS:
         dy, dx = q
         if not dy:
             add("near", coarse, cf, cf, q, columns_of(coarse, dx, 2), middle)
-            for path, (count, skip) in enumerate(((5, 0), (4, 5), (4, 9))):
+            for path, (count, skip) in enumerate(((4, 0), (3, 4), (3, 7), (3, 10))):
                 add("cw", coarse, cw, cw, q, columns_of(coarse, dx, count, skip), middle, (path,))
-            for path, skip in enumerate((2, 6, 10)):
-                add("far", coarse, cf, cf, q, columns_of(coarse, dx, 4, skip), middle, (path,))
+            for path, skip in enumerate((2, 5, 8, 11)):
+                add("far", coarse, cf, cf, q, columns_of(coarse, dx, 3, skip), middle, (path,))
         elif not dx:
             place = coarse_rows(dy, LEVELS - 1)
             add("cw", coarse, cw, cw, q, (coarse.halo, coarse.halo, coarse.columns), place)
@@ -206,39 +220,48 @@
                 name = "far" if skip else "near"
                 add(name, coarse, cf, cf, q, columns_of(coarse, dx, count, skip), coarse_rows(dy, depth))
 
-    first = {}
-    for key in sorted(copies, key=lambda k: (k[0], DIRS.index(k[1]))):
-        first[key] = counter[0]
-        counter[0] += len(copies[key])
-
-    def copies_of(name, q, arriving):
+    groups = (("u", "w", "f"), ("cw", "far", "near"), ("y",))
+    relayed = ("w", "f", "cw", "far", "y")
+
+    def place_of(name, q):
+        group = [name in names for names in groups].index(True)
+        return group * len(DIRS) + DIRS.index(q)
+
+    def wait(sem, count):
+        rows_of = u.at[pl.ds(0, count), :]
+        pltpu.make_async_copy(rows_of, rows_of, sem).wait()
+
+    def total(names, q, path=None):
+        return sum(n for (name, d, way), n in volume.items() if name in names and d == q and path in (None, way))
+
+    def copies_of(name, q):
         back = (-q[0], -q[1])
-        for i, (here, there, path, relay) in enumerate(copies[name, back if arriving else q]):
+        for here, there, path, relay in copies[name, q]:
             yield path, pltpu.make_async_remote_copy(
                 src_ref=here,
                 dst_ref=there,
-                send_sem=send_sem.at[first[name, q] + i],
-                recv_sem=recv_sem.at[first[name, q if arriving else back] + i],
+                send_sem=send_sem.at[place_of(name, q)],
+                recv_sem=recv_sem.at[place_of(name, back)],
                 device_id=name_of(q),
                 device_id_type=MESH,
             )
 
-    def legs_of(name, q):
+    def legs_of(name, q, way=None):
         back = (-q[0], -q[1])
-        for i, (here, there, path, relay) in enumerate(copies[name, q]):
-            if path:
-                yield path, pltpu.make_async_remote_copy(
+        for here, there, path, relay in copies[name, q]:
+            if path and way in (None, path):
+                yield pltpu.make_async_remote_copy(
                     src_ref=here,
                     dst_ref=relay,
-                    send_sem=send_sem.at[first[name, q] + i],
-                    recv_sem=land_sem.at[first[name, q] + i],
+                    send_sem=send_sem.at[place_of(name, q)],
+                    recv_sem=land_sem.at[relayed.index(name)],
                     device_id={"lane": relays[q][path]},
                     device_id_type=MESH,
                 ), pltpu.make_async_remote_copy(
                     src_ref=relay,
                     dst_ref=there,
-                    send_sem=pass_sem.at[first[name, q] + i],
-                    recv_sem=recv_sem.at[first[name, back] + i],
+                    send_sem=pass_sem.at[0],
+                    recv_sem=recv_sem.at[place_of(name, back)],
                     device_id={"lane": ends[q][1]},
                     device_id_type=MESH,
                 )
@@ -251,44 +274,45 @@
 
             @pl.when(ready & (lane == ends[q][0]))
             def _():
-                for path, copy in copies_of(name, q, False):
+                for there, on in legs_of(name, q):
+                    there.start()
+                for path, copy in copies_of(name, q):
                     if not path:
                         copy.start()
-                for path, there, on in legs_of(name, q):
-                    there.start()
 
         @pl.when(direct)
         def _():
-            for path, copy in copies_of(name, q, False):
+            for path, copy in copies_of(name, q):
                 copy.start()
 
-    def pass_on(names, finish=False):
+    def pass_on(names):
         for q in ends:
             for way, relay_lane in relays[q].items():
                 @pl.when(lane == relay_lane)
                 def _():
                     for name in names:
-                        for path, there, on in legs_of(name, q):
-                            if path == way and finish:
-                                on.wait_send()
-                            elif path == way:
-                                there.wait_recv()
+                        if total((name,), q, way):
+                            wait(land_sem.at[relayed.index(name)], total((name,), q, way))
+                            for there, on in legs_of(name, q, way):
                                 on.start()
 
+    def passed_on():
+        for q in ends:
+            for way, relay_lane in relays[q].items():
+                @pl.when(lane == relay_lane)
+                def _():
+                    wait(pass_sem.at[0], total(relayed, q, way))
+
     def sent(names):
-        for name in names:
-            for q in DIRS:
-                @pl.when(exists(q))
-                def _():
-                    for path, copy in copies_of(name, q, False):
-                        copy.wait_send()
+        for q in DIRS:
+            @pl.when(exists(q))
+            def _():
+                wait(send_sem.at[place_of(names[0], q)], total(names, q))
 
     def arrived(names, q, when=None):
         @pl.when(exists(q) if when is None else exists(q) & when)
         def _():
-            for name in names:
-                for path, copy in copies_of(name, q, True):
-                    copy.wait_recv()
+            wait(recv_sem.at[place_of(names[0], q)], total(names, (-q[0], -q[1])))
 
     rows_only, sides, corners = DIRS[:2], DIRS[2:4], DIRS[4:]
 
@@ -422,7 +446,7 @@
     pass_on(("w", "f"))
 
     before = ((u, v), (v, x), (x, v))
-    early_arrived(("u", "w", "f"))
+    early_arrived(groups[0])
     for k, (old, new) in enumerate(before, 1):
         width = 4 * -(-(68 - 2 * k) // 4)
         sweep(fine, old, new, w, f, side(64 - k - width, k), width // 4)
@@ -433,7 +457,7 @@
         start("near", q, jnp.logical_not(late(q)))
     for q in rows_only:
         start("far", q)
-    late_arrived(("u", "w", "f"))
+    late_arrived(groups[0])
     for k, (old, new) in enumerate(before, 1):
         sweep(fine, old, new, w, f, side(64 - k, k - 4), 1)
     restrict(side(30, 0), 1)
@@ -452,8 +476,8 @@
         new = ca if k % 2 == 0 else cb
         inner.append((k, old, new))
         old = new
-    sent(("u", "w", "f", "cw"))
-    early_arrived(("cw", "far", "near"))
+    sent(groups[0])
+    early_arrived(groups[1])
     for k, old, new in inner:
         width = 4 * -(-(48 - 2 * k) // 4)
         sweep(coarse, old, new, cw, cf, side(33 - k - width, k - 1), width // 4)
@@ -461,47 +485,42 @@
     last = inner[-1][2]
     after = ((v, u), (u, v), (v, out))
 
-    def take(column):
-        @pl.loop(0, 3)
+    def take(outer, inner):
+        @pl.loop(0, 2)
         def _(j):
             for p in range(fine.pieces):
-                at = fine.at(column + j, p)
+                at = fine.at(outer + j, p)
                 v[pl.ds(at, SUB), :] = y[pl.ds(at, SUB), :]
 
-    def deliver(at):
-        @pl.loop(0, rows)
-        def _(row):
-            for i in range(4):
-                c = pl.multiple_of(at + SUB * i, SUB)
-                place = pl.multiple_of((row + TOP) * PITCH + MARGIN + c, SUB)
-                out_ref[row, pl.ds(c, SUB), :] = out[pl.ds(place, SUB), :]
-
-    sent(("y", "far", "near"))
-    pass_on(("w", "f", "cw", "far", "y"), finish=True)
-    early_arrived(("y",))
+        for p, s in ((2, 0), (3, 0), (5, 7), (6, 7)):
+            at = (inner + fine.halo) * fine.width + p * SUB + s
+            v[pl.ds(at, 1), :] = y[pl.ds(at, 1), :]
+
+    sent(groups[1])
+    sent(groups[2])
+    passed_on()
+    early_arrived(groups[2])
 
     @pl.loop(0, fine.columns // SUB)
     def _(j):
-        for p, s in ((1, 0), (2, 0), (3, 0), (5, 7), (6, 7), (7, 7)):
+        for p, s in ((1, 0), (2, 0), (6, 7), (7, 7)):
             at = (j * SUB + fine.halo) * fine.width + p * SUB + s
             v[pl.ds(at, SUB, stride=fine.width), :] = y[pl.ds(at, SUB, stride=fine.width), :]
 
-    take(side(-3, 64))
+    take(side(-3, 65), side(-1, 64))
     correct(last, side(-2, 12), 11)
     for m, (old, new) in enumerate(after, 1):
         width = 4 * -(-(43 - 2 * m) // 4)
         sweep(fine, old, new, w, f, side(40 - m - width, 24 + m), width // 4)
-    deliver(side(0, 32))
-
-    late_arrived(("cw", "far", "near"))
+
+    late_arrived(groups[1])
     for k, old, new in inner:
         sweep(coarse, old, new, cw, cf, side(33 - k, k - 17), 4)
-    late_arrived(("y",))
-    take(side(64, -3))
+    late_arrived(groups[2])
+    take(side(65, -3), side(64, -1))
     correct(last, side(20, -2), 7)
     for m, (old, new) in enumerate(after, 1):
         sweep(fine, old, new, w, f, side(40 - m, m - 4), 7)
-    deliver(side(32, 0))
 
 
 def per_device(source_terms, initial_values, absorption):
@@ -514,19 +533,18 @@
 
     shapes = [held(fine.stored * fine.width) for _ in range(9)]
     shapes += [held(coarse.stored * coarse.width) for _ in range(4)]
-    shapes += [held((rows + 2 * TOP) * PITCH), held(2 * 96)]
-    shapes += [held(12 * fine.width), held(8 * coarse.width)]
-    count = 144
+    shapes += [held(2 * 96)]
+    shapes += [held(11 * fine.width), held(6 * coarse.width)]
     shapes += [
         pltpu.SemaphoreType.DMA((3,)),
-        pltpu.SemaphoreType.DMA((count,)),
-        pltpu.SemaphoreType.DMA((count,)),
-        pltpu.SemaphoreType.DMA((count,)),
-        pltpu.SemaphoreType.DMA((count,)),
+        pltpu.SemaphoreType.DMA((3 * len(DIRS),)),
+        pltpu.SemaphoreType.DMA((3 * len(DIRS),)),
+        pltpu.SemaphoreType.DMA((1,)),
+        pltpu.SemaphoreType.DMA((5,)),
     ]
-    return pl.pallas_call(
+    pitched = pl.pallas_call(
         functools.partial(kernel, fine, coarse),
-        out_shape=jax.ShapeDtypeStruct(source_terms.shape, jnp.float32),
+        out_shape=jax.ShapeDtypeStruct(((rows + 2 * TOP) * PITCH, cases), jnp.float32),
         in_specs=[pl.BlockSpec(memory_space=pltpu.HBM)] * 3,
         out_specs=pl.BlockSpec(memory_space=pltpu.VMEM),
         scratch_shapes=shapes,
@@ -534,6 +552,13 @@
             collective_id=0, has_side_effects=True, vmem_limit_bytes=52 * 1024 * 1024
         ),
     )(*[pltpu.with_memory_space_constraint(x, pltpu.HBM) for x in (source_terms, initial_values, absorption)])
+    return pl.pallas_call(
+        deliver,
+        out_shape=jax.ShapeDtypeStruct(source_terms.shape, jnp.float32),
+        in_specs=[pl.BlockSpec(memory_space=pltpu.VMEM)],
+        out_specs=pl.BlockSpec(memory_space=pltpu.HBM),
+        scratch_shapes=[pltpu.SemaphoreType.DMA],
+    )(pitched)
 
 
 def solution(mesh):

time: 66.8 us -> 60 us (0.90)
  Pallas kernels: 63.4 us -> 59.8 us
  local copies, waits for them, and re-layouts: 3.16 us -> 0 us
    pallas_call x1, Pallas kernels: 63.4 us -> 56.5 us  [per_device(): pl.pallas_call(functools.partial(kernel, fine, coarse), out_shape=jax.Sha...]
    pallas_call x0 -> x1, Pallas kernels: none -> 3.24 us  [per_device(): pl.pallas_call(deliver, out_shape=jax.ShapeDtypeStruct(source_terms.shape...]
    unnamed x1 -> x0, local copies, waits for them, and re-layouts: 3.16 us -> none
where the time goes in v3:
time: 60 us; the launch traced here: 59.8 us
  Pallas kernels  59.8 us (100%)
    pallas_call x1, Pallas kernels, per_device(): pl.pallas_call(functools.partial(kernel, fine, coarse), out_shape=jax.Sha...  56.5 us
    pallas_call x1, Pallas kernels, per_device(): pl.pallas_call(deliver, out_shape=jax.ShapeDtypeStruct(source_terms.shape...  3.24 us

profile of v3, /device:TPU:30, one launch (start us, length us, event | category | flops | bytes accessed | tf_op | source)
XLA Modules:
  0.0 59.8 jit_solution(15026038213441703971)
XLA Ops:
  0.0 56.5 %shard_map.37.held = f32[6336,128]{1,0:T(8,128)} custom-call(f32[64,64,128]{2,1,0:T(8,128)} %src_hbm.1, f32[64,64,128]{2,1,0:T(8,128)} %init_hbm.1, f32[64,64,128]{2,1,0:T(8,128)} %abs_hbm.1), custom_call_target="tpu_custom_call" | custom-call | tf_op jit(solution)/shard_map/pallas_call | solution.py:545
  56.6 3.2 %shard_map.38 = f32[64,64,128]{2,1,0:T(8,128)} custom-call(f32[6336,128]{1,0:T(8,128)} %shard_map.37.held), custom_call_target="tpu_custom_call" | custom-call | tf_op jit(solution)/shard_map/pallas_call | solution.py:555

commit v4 on v3

--- a/solution.py
+++ b/solution.py
@@ -138,6 +138,9 @@
             return g.halo + g.columns - depth - skip, g.halo - depth - skip, depth
         return g.halo + skip, g.halo + g.columns + skip, depth
 
+    def outside(g, dx, depth, skip):
+        return g.halo + g.columns + skip if dx > 0 else g.halo - depth - skip
+
     def fine_rows(dy, depth, skip=0):
         if dy > 0:
             return [((5 - depth - skip, 7), (4 - depth - skip, 0), (depth, 1))]
@@ -157,7 +160,7 @@
     middle = [((0, 2), (0, 2), (SUB, 4))]
 
     copies, used, volume = {}, {}, {}
-    offsets = {"w": 0, "f": 3, "y": 9, "cw": 0, "far": 3}
+    offsets = {"w": 0, "f": 9, "y": 18, "cw": 0, "far": 8}
 
     def add(name, g, source, target, q, columns, places, paths=(0,)):
         from_column, to_column, count = columns
@@ -183,15 +186,13 @@
             if not dy and name == "u":
                 add(name, fine, source, target, q, columns_of(fine, dx, depth), own)
             elif not dy:
-                path = 1 if name == "w" else 2
-                add(name, fine, source, target, q, columns_of(fine, dx, 2), own, (path,))
-                add(name, fine, source, target, q, columns_of(fine, dx, 1, 2), own, (3,))
+                add(name, fine, source, target, q, columns_of(fine, dx, 3), own, (2 if name == "w" else 2,))
             elif not dx:
                 add(name, fine, source, target, q, (fine.halo, fine.halo, fine.columns), fine_rows(dy, depth))
             else:
                 add(name, fine, source, target, q, columns_of(fine, dx, corner), fine_rows(dy, corner))
         if not dy:
-            add("y", fine, v, y, q, columns_of(fine, dx, 2, 1), own, (1, 0, 3))
+            add("y", fine, v, y, q, columns_of(fine, dx, 2, 1), own, (2, 0, 2))
         elif not dx:
             add("y", fine, v, y, q, (fine.halo, fine.halo, fine.columns), fine_rows(dy, 2, 1))
         else:
@@ -201,10 +202,10 @@
         dy, dx = q
         if not dy:
             add("near", coarse, cf, cf, q, columns_of(coarse, dx, 2), middle)
-            for path, (count, skip) in enumerate(((4, 0), (3, 4), (3, 7), (3, 10))):
+            for path, count, skip in ((0, 4, 0), (1, 3, 4), (2, 3, 7), (3, 3, 10)):
                 add("cw", coarse, cw, cw, q, columns_of(coarse, dx, count, skip), middle, (path,))
-            for path, skip in enumerate((2, 5, 8, 11)):
-                add("far", coarse, cf, cf, q, columns_of(coarse, dx, 3, skip), middle, (path,))
+            for path, count, skip in ((0, 3, 2), (1, 3, 5), (2, 3, 8), (3, 3, 11)):
+                add("far", coarse, cf, cf, q, columns_of(coarse, dx, count, skip), middle, (path,))
         elif not dx:
             place = coarse_rows(dy, LEVELS - 1)
             add("cw", coarse, cw, cw, q, (coarse.halo, coarse.halo, coarse.columns), place)
@@ -214,20 +215,27 @@
             at = coarse.halo + side(0, 2)
             add("far", coarse, cf, cf, q, (at, at, coarse.columns - 2), place)
         else:
+            add("near", coarse, cf, cf, q, columns_of(coarse, dx, 2), coarse_rows(dy, LEVELS - 1))
             for count, skip, depth in ((2, 0, 12), (3, 2, 10), (4, 5, 7), (3, 9, 3)):
-                add("cw", coarse, cw, cw, q, columns_of(coarse, dx, count, skip), coarse_rows(dy, depth))
-            for count, skip, depth in ((2, 0, 13), (3, 2, 11), (4, 5, 8), (4, 9, 4)):
-                name = "far" if skip else "near"
-                add(name, coarse, cf, cf, q, columns_of(coarse, dx, count, skip), coarse_rows(dy, depth))
-
-    groups = (("u", "w", "f"), ("cw", "far", "near"), ("y",))
+                at = outside(coarse, dx, count, skip)
+                add("turn", coarse, cw, cw, q, (at, at, count), coarse_rows(dy, depth))
+            for count, skip, depth in ((3, 2, 11), (4, 5, 8), (4, 9, 4)):
+                at = outside(coarse, dx, count, skip)
+                add("turn", coarse, cf, cf, q, (at, at, count), coarse_rows(dy, depth))
+
+    groups = (("u", "w", "f"), ("cw", "far"), ("y",), ("near",), ("turn",))
     relayed = ("w", "f", "cw", "far", "y")
 
     def place_of(name, q):
         group = [name in names for names in groups].index(True)
         return group * len(DIRS) + DIRS.index(q)
 
+    def from_side(name, q):
+        return (-q[0], q[1]) if name == "turn" else (-q[0], -q[1])
+
     def wait(sem, count):
+        if not count:
+            return
         rows_of = u.at[pl.ds(0, count), :]
         pltpu.make_async_copy(rows_of, rows_of, sem).wait()
 
@@ -235,14 +243,13 @@
         return sum(n for (name, d, way), n in volume.items() if name in names and d == q and path in (None, way))
 
     def copies_of(name, q):
-        back = (-q[0], -q[1])
         for here, there, path, relay in copies[name, q]:
             yield path, pltpu.make_async_remote_copy(
                 src_ref=here,
                 dst_ref=there,
                 send_sem=send_sem.at[place_of(name, q)],
-                recv_sem=recv_sem.at[place_of(name, back)],
-                device_id=name_of(q),
+                recv_sem=recv_sem.at[place_of(name, from_side(name, q))],
+                device_id=name_of((q[0], 0) if name == "turn" else q),
                 device_id_type=MESH,
             )
 
@@ -312,7 +319,7 @@
     def arrived(names, q, when=None):
         @pl.when(exists(q) if when is None else exists(q) & when)
         def _():
-            wait(recv_sem.at[place_of(names[0], q)], total(names, (-q[0], -q[1])))
+            wait(recv_sem.at[place_of(names[0], q)], total(names, from_side(names[0], q)))
 
     rows_only, sides, corners = DIRS[:2], DIRS[2:4], DIRS[4:]
 
@@ -441,7 +448,7 @@
     for name in ("u", "w", "f"):
         for q in rows_only:
             start(name, q)
-    for q in sides + corners + rows_only:
+    for q in sides + rows_only:
         start("cw", q)
     pass_on(("w", "f"))
 
@@ -451,7 +458,7 @@
         width = 4 * -(-(68 - 2 * k) // 4)
         sweep(fine, old, new, w, f, side(64 - k - width, k), width // 4)
     restrict(side(0, 2), 15)
-    for q in sides + corners:
+    for q in sides:
         start("far", q)
     for q in sides + corners:
         start("near", q, jnp.logical_not(late(q)))
@@ -477,7 +484,15 @@
         inner.append((k, old, new))
         old = new
     sent(groups[0])
-    early_arrived(groups[1])
+    for q in rows_only:
+        arrived(groups[1], q)
+    for q in sides:
+        arrived(groups[1], q, jnp.logical_not(late(q)))
+    for q in corners:
+        start("turn", q, jnp.logical_not(late(q)))
+    early_arrived(groups[3])
+    for q in corners:
+        arrived(groups[4], q, jnp.logical_not(late(q)))
     for k, old, new in inner:
         width = 4 * -(-(48 - 2 * k) // 4)
         sweep(coarse, old, new, cw, cf, side(33 - k - width, k - 1), width // 4)
@@ -496,8 +511,12 @@
             at = (inner + fine.halo) * fine.width + p * SUB + s
             v[pl.ds(at, 1), :] = y[pl.ds(at, 1), :]
 
-    sent(groups[1])
-    sent(groups[2])
+    for q in sides:
+        arrived(groups[1], q, late(q))
+    for q in corners:
+        start("turn", q, late(q))
+    for names in groups[1:4]:
+        sent(names)
     passed_on()
     early_arrived(groups[2])
 
@@ -513,7 +532,10 @@
         width = 4 * -(-(43 - 2 * m) // 4)
         sweep(fine, old, new, w, f, side(40 - m - width, 24 + m), width // 4)
 
-    late_arrived(groups[1])
+    late_arrived(groups[3])
+    for q in corners:
+        arrived(groups[4], q, late(q))
+    sent(groups[4])
     for k, old, new in inner:
         sweep(coarse, old, new, cw, cf, side(33 - k, k - 17), 4)
     late_arrived(groups[2])
@@ -534,11 +556,11 @@
     shapes = [held(fine.stored * fine.width) for _ in range(9)]
     shapes += [held(coarse.stored * coarse.width) for _ in range(4)]
     shapes += [held(2 * 96)]
-    shapes += [held(11 * fine.width), held(6 * coarse.width)]
+    shapes += [held(22 * fine.width), held(16 * coarse.width)]
     shapes += [
         pltpu.SemaphoreType.DMA((3,)),
-        pltpu.SemaphoreType.DMA((3 * len(DIRS),)),
-        pltpu.SemaphoreType.DMA((3 * len(DIRS),)),
+        pltpu.SemaphoreType.DMA((5 * len(DIRS),)),
+        pltpu.SemaphoreType.DMA((5 * len(DIRS),)),
         pltpu.SemaphoreType.DMA((1,)),
         pltpu.SemaphoreType.DMA((5,)),
     ]

time: 60 us -> 59.5 us (level)
  no operation moved by 1% of the time
where the time goes in v4:
time: 59.5 us; the launch traced here: 59.3 us
  Pallas kernels  59.3 us (100%)
    pallas_call x1, Pallas kernels, per_device(): pl.pallas_call(functools.partial(kernel, fine, coarse), out_shape=jax.Sha...  56.1 us
    pallas_call x1, Pallas kernels, per_device(): pl.pallas_call(deliver, out_shape=jax.ShapeDtypeStruct(source_terms.shape...  3.24 us

profile of v4, /device:TPU:30, one launch (start us, length us, event | category | flops | bytes accessed | tf_op | source)
XLA Modules:
  0.0 59.3 jit_solution(5508287923702923932)
XLA Ops:
  0.0 56.1 %shard_map.37.held = f32[6336,128]{1,0:T(8,128)} custom-call(f32[64,64,128]{2,1,0:T(8,128)} %src_hbm.1, f32[64,64,128]{2,1,0:T(8,128)} %init_hbm.1, f32[64,64,128]{2,1,0:T(8,128)} %abs_hbm.1), custom_call_target="tpu_custom_call" | custom-call | tf_op jit(solution)/shard_map/pallas_call | solution.py:567
  56.1 3.2 %shard_map.38 = f32[64,64,128]{2,1,0:T(8,128)} custom-call(f32[6336,128]{1,0:T(8,128)} %shard_map.37.held), custom_call_target="tpu_custom_call" | custom-call | tf_op jit(solution)/shard_map/pallas_call | solution.py:577

commit v5 on v4

--- a/solution.py
+++ b/solution.py
@@ -349,7 +349,7 @@
         return found
 
     def sweep(g, old, new, weight, load, at, blocks):
-        @pl.loop(0, blocks)
+        @pl.loop(0, blocks, unroll=2 if blocks % 2 == 0 else 1)
         def _(b):
             column = at + BLOCK * b
             for p in range(g.pieces):

time: 59.5 us -> 59.2 us (level)
  no operation moved by 1% of the time
where the time goes in v5:
time: 59.2 us; the launch traced here: 59 us
  Pallas kernels  59 us (100%)
    pallas_call x1, Pallas kernels, per_device(): pl.pallas_call(functools.partial(kernel, fine, coarse), out_shape=jax.Sha...  55.7 us
    pallas_call x1, Pallas kernels, per_device(): pl.pallas_call(deliver, out_shape=jax.ShapeDtypeStruct(source_terms.shape...  3.24 us

profile of v5, /device:TPU:30, one launch (start us, length us, event | category | flops | bytes accessed | tf_op | source)
XLA Modules:
  0.0 59.0 jit_solution(11010058322156155597)
XLA Ops:
  0.0 55.7 %shard_map.37.held = f32[6336,128]{1,0:T(8,128)} custom-call(f32[64,64,128]{2,1,0:T(8,128)} %src_hbm.1, f32[64,64,128]{2,1,0:T(8,128)} %init_hbm.1, f32[64,64,128]{2,1,0:T(8,128)} %abs_hbm.1), custom_call_target="tpu_custom_call" | custom-call | tf_op jit(solution)/shard_map/pallas_call | solution.py:567
  55.8 3.2 %shard_map.38 = f32[64,64,128]{2,1,0:T(8,128)} custom-call(f32[6336,128]{1,0:T(8,128)} %shard_map.37.held), custom_call_target="tpu_custom_call" | custom-call | tf_op jit(solution)/shard_map/pallas_call | solution.py:577
